TPU v7x, 8 devices: a whole 2x2x1 slice. The times are simulated.
8 devices in a mesh: dp: 1 (over z), wg: 8 (over y, x, core).
Axes of the slice: x: 2, y: 2, z: 1, core: 2. Of those that a mesh axis runs over, the one named last changes fastest.
Arguments:
- hidden: bfloat16 [32, 384, 6144], P(('dp', 'wg'))
- seq_lens: int32 [32], P(('dp', 'wg'))
- route_idx: int32 [12288, 2], P(('dp', 'wg'))
- g_attn_in: bfloat16 [6144], P('wg')
- w_query: bfloat16 [6144, 6144], P('wg')
- w_key: bfloat16 [6144, 1024], P('wg')
- w_value: bfloat16 [6144, 1024], P('wg')
- w_attn_out: bfloat16 [6144, 6144], P('wg')
- g_attn_out: bfloat16 [6144], P('wg')
- g_moe_in: bfloat16 [6144], P('wg')
- w_router: bfloat16 [6144, 8], P('wg')
- w_gate: bfloat16 [8, 6144, 1024], P(None, 'wg')
- w_up: bfloat16 [8, 6144, 1024], P(None, 'wg')
- w_down: bfloat16 [8, 1024, 6144], P(None, 'wg')
- g_moe_out: bfloat16 [6144], P('wg')
Outputs:
- output 1: bfloat16 [32, 384, 6144], P(('dp', 'wg'))
- output 2: bfloat16 [32, 384, 8, 128], P(('dp', 'wg'))
- output 3: bfloat16 [32, 384, 8, 128], P(('dp', 'wg'))
All inputs are finite; a program needn't handle non-finite values.
Results may differ from a plain program's by a relative error of at most 0.02.
Values are sent between devices in bfloat16 or wider.
A program may use at most 1 GiB of HBM per device.

v0:
```python
import functools
import jax
import jax.numpy as jnp
from jax import lax
from jax.sharding import PartitionSpec as P

HEAD_DIM = 128
SOFT_CAP = 30.0
NORM_EPS = 1e-5
ROPE_BASE = 10000.0
ATTN_SCALE = HEAD_DIM ** -0.5


def dot_f32(left_op, right_op):
    return jnp.dot(left_op, right_op, preferred_element_type=jnp.float32)


def rms_norm(values, gain_vec):
    values_f32 = values.astype(jnp.float32)
    inv_rms = lax.rsqrt(jnp.mean(values_f32 * values_f32, axis=-1, keepdims=True) + NORM_EPS)
    return values_f32 * inv_rms * gain_vec.astype(jnp.float32)


def rope_tables(seq_len):
    half_dim = HEAD_DIM // 2
    inv_freq = ROPE_BASE ** (-jnp.arange(half_dim, dtype=jnp.float32) * (2.0 / HEAD_DIM))
    angles = jnp.arange(seq_len, dtype=jnp.float32)[:, None] * inv_freq[None, :]
    return jnp.cos(angles)[:, None, :], jnp.sin(angles)[:, None, :]


def apply_rope(values, cos_t, sin_t):
    half_dim = HEAD_DIM // 2
    values_f32 = values.astype(jnp.float32)
    first_half = values_f32[..., :half_dim]
    second_half = values_f32[..., half_dim:]
    return jnp.concatenate([first_half * cos_t - second_half * sin_t, second_half * cos_t + first_half * sin_t], axis=-1).astype(jnp.bfloat16)


def attend_prompt(operands):
    q_rows, k_rows, v_rows, length = operands
    positions = jnp.arange(q_rows.shape[0])
    scores = jnp.einsum('qkgd,skd->kgqs', q_rows, k_rows, preferred_element_type=jnp.float32) * ATTN_SCALE
    scores = SOFT_CAP * jnp.tanh(scores / SOFT_CAP)
    allowed = (positions[None, :] <= positions[:, None]) & (positions[None, :] < length)
    scores = jnp.where(allowed, scores, -1e30)
    attn_probs = jax.nn.softmax(scores, axis=-1).astype(jnp.bfloat16)
    return jnp.einsum('kgqs,skd->qkgd', attn_probs, v_rows, preferred_element_type=jnp.float32).astype(jnp.bfloat16)


def attend_rows(q_proj, k_proj, v_proj, seq_lens):
    n_prompts = seq_lens.shape[0]
    seq_len = q_proj.shape[0] // n_prompts
    n_heads = q_proj.shape[1] // HEAD_DIM
    n_kv = k_proj.shape[1] // HEAD_DIM
    cos_t, sin_t = rope_tables(seq_len)
    q_rope = apply_rope(q_proj.reshape(n_prompts, seq_len, n_heads, HEAD_DIM), cos_t, sin_t)
    k_rope = apply_rope(k_proj.reshape(n_prompts, seq_len, n_kv, HEAD_DIM), cos_t, sin_t)
    v_heads = v_proj.reshape(n_prompts, seq_len, n_kv, HEAD_DIM)
    q_groups = q_rope.reshape(n_prompts, seq_len, n_kv, n_heads // n_kv, HEAD_DIM)
    context = lax.map(attend_prompt, (q_groups, k_rope, v_heads, seq_lens))
    return context.reshape(n_prompts * seq_len, n_heads * HEAD_DIM), k_rope, v_heads


def moe_rows(h_moe, gate_probs, route_idx, w_gate, w_up, w_down):
    top_k = route_idx.shape[1]
    flat_ids = route_idx.reshape(-1)
    pair_order = jnp.argsort(flat_ids, stable=True)
    counts = jnp.bincount(flat_ids, length=w_gate.shape[0]).astype(jnp.int32)
    sorted_rows = jnp.take(h_moe, pair_order // top_k, axis=0)
    gate_act = lax.ragged_dot(sorted_rows, w_gate, counts, preferred_element_type=jnp.float32)
    up_act = lax.ragged_dot(sorted_rows, w_up, counts, preferred_element_type=jnp.float32)
    inner_act = (jax.nn.gelu(gate_act) * up_act).astype(jnp.bfloat16)
    expert_out = lax.ragged_dot(inner_act, w_down, counts, preferred_element_type=jnp.float32)
    pair_out = jnp.take(expert_out, jnp.argsort(pair_order), axis=0).reshape(h_moe.shape[0], top_k, -1)
    return jnp.sum(gate_probs[:, :, None] * pair_out, axis=1)


def solution(mesh):
    row_spec = P(('dp', 'wg'))
    dim0_spec = P('wg', None)
    dim1_spec = P(None, 'wg', None)
    gather_dim0 = functools.partial(lax.all_gather, axis_name='wg', axis=0, tiled=True)
    gather_dim1 = functools.partial(lax.all_gather, axis_name='wg', axis=1, tiled=True)

    def device_fn(hidden, seq_lens, route_idx, g_attn_in, w_query, w_key, w_value, w_attn_out, g_attn_out, g_moe_in, w_router, w_gate, w_up, w_down, g_moe_out):
        n_prompts, seq_len, d_model = hidden.shape
        tok_rows = hidden.reshape(n_prompts * seq_len, d_model)
        h_attn = rms_norm(tok_rows, gather_dim0(g_attn_in)).astype(jnp.bfloat16)
        q_proj = dot_f32(h_attn, gather_dim0(w_query)).astype(jnp.bfloat16)
        k_proj = dot_f32(h_attn, gather_dim0(w_key)).astype(jnp.bfloat16)
        v_proj = dot_f32(h_attn, gather_dim0(w_value)).astype(jnp.bfloat16)
        context_rows, k_rope, v_heads = attend_rows(q_proj, k_proj, v_proj, seq_lens)
        attn_out = dot_f32(context_rows, gather_dim0(w_attn_out))
        mid_rows = (tok_rows.astype(jnp.float32) + rms_norm(attn_out, gather_dim0(g_attn_out))).astype(jnp.bfloat16)
        h_moe = rms_norm(mid_rows, gather_dim0(g_moe_in)).astype(jnp.bfloat16)
        router_probs = jax.nn.softmax(dot_f32(h_moe, gather_dim0(w_router)), axis=-1)
        gate_probs = jnp.take_along_axis(router_probs, route_idx, axis=1)
        moe_out = moe_rows(h_moe, gate_probs, route_idx, gather_dim1(w_gate), gather_dim1(w_up), gather_dim1(w_down))
        y_rows = (mid_rows.astype(jnp.float32) + rms_norm(moe_out, gather_dim0(g_moe_out))).astype(jnp.bfloat16)
        return y_rows.reshape(hidden.shape), k_rope, v_heads

    return jax.shard_map(
        device_fn,
        mesh=mesh,
        in_specs=(row_spec, row_spec, row_spec, P('wg'), dim0_spec, dim0_spec, dim0_spec, dim0_spec, P('wg'), P('wg'), dim0_spec, dim1_spec, dim1_spec, dim1_spec, P('wg')),
        out_specs=(row_spec, row_spec, row_spec),
        check_vma=False,
    )
```

profile of v0, /device:TPU:0, one launch (start us, length us, event | category | flops | bytes accessed | tf_op | source)
XLA Modules:
  0.0 2680.6 jit_solution(17419775579785677998)
XLA Ops:
  12.0 13.7 all-gather
  33.8 10.8 all-gather.1
  45.3 10.9 all-gather.2
  59.5 22.2 scatter_custom_fusion
  96.4 10.9 all-gather.3
  107.9 11.7 all_gather.43
  122.2 16.8 fusion.35
  139.0 23.8 convert_bitcast_fusion.1
  167.0 24.3 fusion.46
  199.7 285.7 %all-gather.16.cloned.1.call-done = bf16[6144,6144]{1,0:T(8,128)(2,1)} async-done(((bf16[768,6144]{1,0:T(8,128)(2,1)}), bf16[6144,6144]{1,0:T(8,128)(2,1)}) %all-gather.16.cloned.1.call-update) | async-done | bytes 75497488 | tf_op jit(solution)/shard_map/all_gather | solution.py:89
  485.4 135.3 %convert_bitcast_fusion = f32[192,8,48,128]{3,1,2,0:T(8,128)} fusion(bf16[1536,6144]{1,0:T(8,128)(2,1)} %fusion.35, bf16[6144,6144]{1,0:T(8,128)(2,1)} %all-gather.16.cloned.1.call-done), kind=kOutput, calls=%fused_computation.49 | convolution fusion | flops 115982991360 | bytes 132120576 | tf_op jit(solution)/shard_map/dot_general | solution.py:15
  620.7 32.9 %copy.68 = f32[192,8,48,128]{3,2,1,0:T(8,128)} copy(f32[192,8,48,128]{3,1,2,0:T(8,128)} %convert_bitcast_fusion) | data formatting | bytes 75497472
  653.6 32.8 %subtract_convert_fusion = (bf16[4,384,48,64]{3,2,1,0:T(8,128)(2,1)S(1)}, bf16[4,384,48,64]{3,2,1,0:T(8,128)(2,1)}) fusion(f32[4,384,48,128]{3,2,1,0:T(8,128)} %bitcast.109, f32[384,64]{1,0:T(8,128)S(1)} %copy-done.7, f32[384,64]{1,0:T(8,128)S(1)} %copy-done.5), kind=kLoop, calls=%fused_computation.53 | loop fusion | flops 37748736 | bytes 56819712 | tf_op jit(solution)/shard_map/convert.8
  686.4 15.8 copy.51
  702.1 12.5 copy.52
  714.6 12.4 pad_maximum_fusion
  727.0 185.4 %while.12 = (s32[]{:T(128)}, bf16[4,384,8,6,128]{1,4,3,2,0:T(8,128)(2,1)}, bf16[4,384,8,128]{3,2,1,0:T(8,128)(2,1)}, s32[4]{0:T(128)S(1)}, bf16[4,384,8,128]{3,2...) while((s32[]{:T(128)}, bf16[4,384,8,6,128]{1,4,3,2,0:T(8,128)(2,1)}, ...), condition=%wide.region_4.5_spmd, body=%wide.region_1.4_spmd.sunk | while | flops 5516348416 | bytes 78448992 | solution.py:60
  730.0 12.5 fusion.81
  742.5 13.6 fusion.82
  756.6 16.9 bitcast_dynamic-update-slice_fusion.2
  776.3 12.5 fusion.81
  788.8 13.6 fusion.82
  802.9 16.9 bitcast_dynamic-update-slice_fusion.2
  822.6 12.5 fusion.81
  835.1 13.6 fusion.82
  849.2 16.9 bitcast_dynamic-update-slice_fusion.2
  868.9 12.5 fusion.81
  881.4 13.6 fusion.82
  895.5 16.9 bitcast_dynamic-update-slice_fusion.2
  912.4 21.7 copy.55
  944.7 138.4 %multiply_reduce_fusion.2 = (f32[1536]{0:T(1024)S(1)}, f32[1536,6144]{1,0:T(8,128)}) fusion(bf16[1536,6144]{0,1:T(8,128)(2,1)} %bitcast.114, bf16[6144,6144]{1,0:T(8,128)(2,1)} %all-gather.18.cloned.1.call-done), kind=kOutput, calls=%fused_computation.51 | convolution fusion | flops 115982991360 | bytes 132126720 | tf_op jit(solution)/shard_map/dot_general | solution.py:15
  1083.1 27.9 %fusion.29 = (f32[1536]{0:T(1024)S(1)}, bf16[1536,6144]{1,0:T(8,128)(2,1)}) fusion(f32[6144]{0:T(1024)S(1)} %bitcast.118, f32[1536,6144]{1,0:T(8,128)} %get-tuple-element.144, f32[1536]{0:T(1024)S(1)} %add_rsqrt_fusion.2, bf16[4,384,6144]{2,1,0:T(8,128)(2,1)} %param.17), kind=kLoop, calls=%fused_computation.38 | loop fusion | flops 75495936 | bytes 75534336 | tf_op jit(solution)/shard_map/reduce_sum | solution.py:20
  1111.1 11.7 fusion.31
  1129.3 18.2 gather_fusion.2
  1149.8 70.7 %gather_fusion = bf16[3072,6144]{1,0:T(8,128)(2,1)} fusion(bf16[1536,6144]{1,0:T(8,128)(2,1)} %copy-done, s32[3072]{0:T(1024)S(1)} %copy-done.16), kind=kCustom, calls=%fused_computation | custom fusion | bytes 75509760 | tf_op jit(solution)/shard_map/jit(_take)/gather | solution.py:69
  1220.4 25.5 broadcast_select_fusion
  1245.9 16.3 all-gather.20.cloned.1.call-done
  1262.2 84.6 %ragged-dot-none.2 = f32[3072,1024]{1,0:T(8,128)} custom-call(s32[1]{0:T(128)} %get-tuple-element.85, s32[9]{0:T(128)} %get-tuple-element.86, s32[19]{0:T(128)} %get-tuple-element.87, s32[19]{0:T(128)} %get-tuple-element.88, s32[1]{0:T(128)} %get-tuple-element.85, bf16[3072,6144]{1,0:T(8,128)(2,1)} %broadcast_select_fusion, ...), custom_call_target="tpu_custom_call" | custom-call | flops 38654705664 | bytes 150994976 | tf_op jit(solution)/shard_map/ragged_dot_general/ragged-dot-none
  1346.8 356.9 %all-gather.22.cloned.1.call-done = bf16[8,6144,1024]{2,1,0:T(8,128)(2,1)} async-done(((bf16[8,768,1024]{2,1,0:T(8,128)(2,1)}), bf16[8,6144,1024]{2,1,0:T(8,128)(2,1)}) %all-gather.22.cloned.1.call-update) | async-done | bytes 100663312 | tf_op jit(solution)/shard_map/all_gather | solution.py:98
  1703.6 84.5 %ragged-dot-none.1 = f32[3072,1024]{1,0:T(8,128)} custom-call(s32[1]{0:T(128)} %get-tuple-element.85, s32[9]{0:T(128)} %get-tuple-element.86, s32[19]{0:T(128)} %get-tuple-element.87, s32[19]{0:T(128)} %get-tuple-element.88, s32[1]{0:T(128)} %get-tuple-element.85, bf16[3072,6144]{1,0:T(8,128)(2,1)} %broadcast_select_fusion, ...), custom_call_target="tpu_custom_call" | custom-call | flops 38654705664 | bytes 150994976 | tf_op jit(solution)/shard_map/ragged_dot_general/ragged-dot-none
  1788.1 12.8 fusion.45
  1800.9 344.4 %all-gather.24.cloned.1.call-done = bf16[8,1024,6144]{2,1,0:T(8,128)(2,1)} async-done(((bf16[8,128,6144]{2,1,0:T(8,128)(2,1)}), bf16[8,1024,6144]{2,1,0:T(8,128)(2,1)}) %all-gather.24.cloned.1.call-update) | async-done | bytes 100663312 | tf_op jit(solution)/shard_map/all_gather | solution.py:98
  2145.3 99.0 %ragged-dot-none = f32[3072,6144]{1,0:T(8,128)} custom-call(s32[1]{0:T(128)} %get-tuple-element.85, s32[9]{0:T(128)} %get-tuple-element.86, s32[19]{0:T(128)} %get-tuple-element.87, s32[19]{0:T(128)} %get-tuple-element.88, s32[1]{0:T(128)} %get-tuple-element.85, bf16[3072,1024]{1,0:T(8,128)(2,1)} %fusion.45, bf16[8,1024,6144]{2,1,0:T(8,128)(2,1)} %all-gather.24.cloned.1.call-done), custom_call_target="tpu_custom_call" | custom-call | flops 38654705664 | bytes 182452256 | tf_op jit(solution)/shard_map/ragged_dot_general/ragged-dot-none
  2244.3 138.4 %gather_fusion.1 = f32[3072,6144]{1,0:T(8,128)} fusion(f32[3072,6144]{1,0:T(8,128)} %ragged-dot-none, s32[3072]{0:T(1024)S(1)} %copy-done.15), kind=kCustom, calls=%fused_computation.1 | custom fusion | bytes 151007232 | tf_op jit(solution)/shard_map/jit(_take)/gather | solution.py:74
  2382.7 83.3 %gather.17 = f32[1536,2,6144]{2,1,0:T(2,128)} reshape(f32[3072,6144]{1,0:T(8,128)} %gather_fusion.1) | data formatting | bytes 150994944 | tf_op jit(solution)/shard_map/jit(_take)/gather | solution.py:74
  2465.9 168.3 %multiply_reduce_fusion = f32[1536,6144]{1,0:T(8,128)} fusion(f32[1536,2,6144]{2,1,0:T(2,128)} %gather.17, pred[1536,2]{1,0:T(8,128)(4,1)S(1)} %copy-done.8, f32[1536,2]{1,0:T(8,128)S(1)} %copy-done.3), kind=kLoop, calls=%fused_computation.34 | loop fusion | flops 47185920 | bytes 113261568 | tf_op jit(solution)/shard_map/reduce_sum | solution.py:75
  2634.3 13.6 multiply_reduce_fusion.1
  2647.9 25.6 fusion.32
  (133 shorter events, 79.9 us)
Async XLA Ops:
  7.2 131.8 %all-gather.14.cloned.1.call-start = ((), (), s32[]{:S(2)}) async-start(), calls=%async_computation.1 | async-start | bytes 14155776 | tf_op jit(solution)/shard_map/all_gather | solution.py:90
  7.9 159.1 %all-gather.12.cloned.1.call-start = ((), (), s32[]{:S(2)}) async-start(), calls=%async_computation | async-start | bytes 14155776 | tf_op jit(solution)/shard_map/all_gather | solution.py:91
  8.6 476.8 %all-gather.16.cloned.1.call-start = ((), (), s32[]{:S(2)}) async-start(), calls=%async_computation.2 | async-start | bytes 84934656 | tf_op jit(solution)/shard_map/all_gather | solution.py:89
  9.4 935.3 %all-gather.18.cloned.1.call-start = ((), (), s32[]{:S(2)}) async-start(), calls=%async_computation.3 | async-start | bytes 84934656 | tf_op jit(solution)/shard_map/all_gather | solution.py:93
  10.0 2.0 copy-start.19
  10.0 1252.2 %all-gather.20.cloned.1.call-start = ((), (), s32[]{:S(2)}) async-start(), calls=%async_computation.4 | async-start | bytes 113246208 | tf_op jit(solution)/shard_map/all_gather | solution.py:98
  10.6 1693.1 %all-gather.22.cloned.1.call-start = ((), (), s32[]{:S(2)}) async-start(), calls=%async_computation.5 | async-start | bytes 113246208 | tf_op jit(solution)/shard_map/all_gather | solution.py:98
  11.1 22.7 copy-start.20
  11.1 34.1 %copy-start.21 = (bf16[768]{0:T(1024)(128)(2,1)S(1)}, bf16[768]{0:T(1024)(128)(2,1)}, u32[]{:S(2)}) copy-start(bf16[768]{0:T(1024)(128)(2,1)} %param.26) | copy-start | bytes 4612
  11.2 45.7 %copy-start.10 = (s32[1536,2]{0,1:T(2,128)S(1)}, s32[1536,2]{0,1:T(2,128)}, u32[]{:S(2)}) copy-start(s32[1536,2]{0,1:T(2,128)} %param.19) | copy-start | bytes 36868
  11.2 85.2 %copy-start.22 = (bf16[768]{0:T(1024)(128)(2,1)S(1)}, bf16[768]{0:T(1024)(128)(2,1)}, u32[]{:S(2)}) copy-start(bf16[768]{0:T(1024)(128)(2,1)} %param.31) | copy-start | bytes 4612
  11.2 96.8 %copy-start.18 = (bf16[768,8]{0,1:T(8,128)(2,1)S(1)}, bf16[768,8]{0,1:T(8,128)(2,1)}, u32[]{:S(2)}) copy-start(bf16[768,8]{0,1:T(8,128)(2,1)} %param.27) | copy-start | bytes 36868
  11.2 2134.1 %all-gather.24.cloned.1.call-start = ((), (), s32[]{:S(2)}) async-start(), calls=%async_computation.6 | async-start | bytes 113246208 | tf_op jit(solution)/shard_map/all_gather | solution.py:98
  122.2 71.5 %copy-start.4 = (f32[384,64]{1,0:T(8,128)}, f32[384,64]{1,0:T(8,128)S(1)}, u32[]{:S(2)}) copy-start(f32[384,64]{1,0:T(8,128)S(1)} %get-tuple-element.141) | copy-start | bytes 294916
  122.2 71.5 %copy-start.6 = (f32[384,64]{1,0:T(8,128)}, f32[384,64]{1,0:T(8,128)S(1)}, u32[]{:S(2)}) copy-start(f32[384,64]{1,0:T(8,128)S(1)} %get-tuple-element.142) | copy-start | bytes 294916
  167.0 26.8 copy-start.2
  620.7 32.9 %copy-start.5 = (f32[384,64]{1,0:T(8,128)S(1)}, f32[384,64]{1,0:T(8,128)}, u32[]{:S(2)}) copy-start(f32[384,64]{1,0:T(8,128)} %copy-done.4) | copy-start | bytes 294916
  620.7 32.9 %copy-start.7 = (f32[384,64]{1,0:T(8,128)S(1)}, f32[384,64]{1,0:T(8,128)}, u32[]{:S(2)}) copy-start(f32[384,64]{1,0:T(8,128)} %copy-done.6) | copy-start | bytes 294916
  714.6 12.4 copy-start.23
  944.7 138.4 %copy-start.13 = (f32[8,1,768]{2,1,0:T(1,128)S(1)}, f32[8,1,768]{2,1,0:T(1,128)}, u32[]{:S(2)}) copy-start(f32[8,1,768]{2,1,0:T(1,128)} %convert_element_type.104) | copy-start | bytes 73732
  1083.1 27.9 %copy-start.14 = (f32[8,1,768]{2,1,0:T(1,128)S(1)}, f32[8,1,768]{2,1,0:T(1,128)}, u32[]{:S(2)}) copy-start(f32[8,1,768]{2,1,0:T(1,128)} %convert_element_type.105) | copy-start | bytes 73732
  1111.0 11.7 copy-start.9
  1122.8 6.4 copy-start
  1122.8 6.5 copy-start.1
  1129.3 19.2 copy-start.11
  1129.3 20.5 copy-start.16
  1149.8 70.7 %copy-start.17 = (pred[3072]{0:T(1024)(128)(4,1)S(1)}, pred[3072]{0:T(1024)(128)(4,1)}, u32[]{:S(2)}) copy-start(pred[3072]{0:T(1024)(128)(4,1)} %compare_and_fusion) | copy-start | bytes 9220
  1800.9 443.4 %copy-start.15 = (s32[3072]{0:T(1024)S(1)}, s32[3072]{0:T(1024)}, u32[]{:S(2)}) copy-start(s32[3072]{0:T(1024)} %fusion.53) | copy-start | bytes 36868
  2382.6 83.3 %copy-start.3 = (f32[1536,2]{1,0:T(8,128)S(1)}, f32[1536,2]{1,0:T(8,128)}, u32[]{:S(2)}) copy-start(f32[1536,2]{1,0:T(8,128)} %copy.58) | copy-start | bytes 36868
  2382.7 83.3 %copy-start.8 = (pred[1536,2]{1,0:T(8,128)(4,1)S(1)}, pred[1536,2]{1,0:T(8,128)(4,1)}, u32[]{:S(2)}) copy-start(pred[1536,2]{1,0:T(8,128)(4,1)} %broadcast_in_dim.76) | copy-start | bytes 9220
  2634.3 13.7 copy-start.12
Sparse Core Ops, SparseCore 0:
  9.8 69.5 all-gather.13
  81.2 68.7 all-gather.11
  151.9 333.5 all-gather.15
  487.1 333.5 all-gather.17
  822.4 439.7 all-gather.19
  1263.9 439.6 all-gather.21
  1705.5 439.7 all-gather.23
where the time goes:
time: 2690 us; the launch traced here: 2680 us
  waiting for transfers between devices  1010 us (38%)
  matrix products  498 us (19%)
  local copies, waits for them, and re-layouts  429 us (16%)
  other arithmetic  403 us (15%)
  Pallas kernels  270 us (10%)
  blocking collectives  58.1 us (2%)
    all_gather x1, waiting for transfers between devices, device_fn(): gather_dim1(w_up)  357 us
    all_gather x1, waiting for transfers between devices, device_fn(): gather_dim1(w_down)  344 us
    dot_general x5, matrix products, dot_f32(): return jnp.dot(left_op, right_op, preferred_element_type=jnp.float32)  327 us
    all_gather x1, waiting for transfers between devices, device_fn(): q_proj = dot_f32(h_attn, gather_dim0(w_query)).astype(jnp.bfloat16)  286 us
    another operation x3, Pallas kernels  268 us
    gather x2, local copies, waits for them, and re-layouts, moe_rows(): jnp.take(expert_out, jnp.argsort(pair_order), axis=0)  222 us
    reduce_sum x1, other arithmetic, moe_rows(): return jnp.sum(gate_probs[:, :, None] * pair_out, axis=1)  168 us
    gather x1, local copies, waits for them, and re-layouts, moe_rows(): sorted_rows = jnp.take(h_moe, pair_order // top_k, axis=0)  70.7 us
  transfers between devices with their start and end apart: 7, of which 4 were waited for; matrix products, arithmetic and copies ran while one was open for 34% of the time, Pallas kernels for 6%

commit v1 on v0

--- a/solution.py
+++ b/solution.py
@@ -61,20 +61,6 @@
     return context.reshape(n_prompts * seq_len, n_heads * HEAD_DIM), k_rope, v_heads
 
 
-def moe_rows(h_moe, gate_probs, route_idx, w_gate, w_up, w_down):
-    top_k = route_idx.shape[1]
-    flat_ids = route_idx.reshape(-1)
-    pair_order = jnp.argsort(flat_ids, stable=True)
-    counts = jnp.bincount(flat_ids, length=w_gate.shape[0]).astype(jnp.int32)
-    sorted_rows = jnp.take(h_moe, pair_order // top_k, axis=0)
-    gate_act = lax.ragged_dot(sorted_rows, w_gate, counts, preferred_element_type=jnp.float32)
-    up_act = lax.ragged_dot(sorted_rows, w_up, counts, preferred_element_type=jnp.float32)
-    inner_act = (jax.nn.gelu(gate_act) * up_act).astype(jnp.bfloat16)
-    expert_out = lax.ragged_dot(inner_act, w_down, counts, preferred_element_type=jnp.float32)
-    pair_out = jnp.take(expert_out, jnp.argsort(pair_order), axis=0).reshape(h_moe.shape[0], top_k, -1)
-    return jnp.sum(gate_probs[:, :, None] * pair_out, axis=1)
-
-
 def solution(mesh):
     row_spec = P(('dp', 'wg'))
     dim0_spec = P('wg', None)
@@ -84,19 +70,44 @@
 
     def device_fn(hidden, seq_lens, route_idx, g_attn_in, w_query, w_key, w_value, w_attn_out, g_attn_out, g_moe_in, w_router, w_gate, w_up, w_down, g_moe_out):
         n_prompts, seq_len, d_model = hidden.shape
+        n_experts = w_gate.shape[0]
+        half = n_experts // 2
         tok_rows = hidden.reshape(n_prompts * seq_len, d_model)
-        h_attn = rms_norm(tok_rows, gather_dim0(g_attn_in)).astype(jnp.bfloat16)
+        small = jnp.concatenate([g_attn_in, g_attn_out, g_moe_in, g_moe_out, w_router.T.reshape(-1)])
+        small = lax.all_gather(small, 'wg', axis=0, tiled=False)
+        n_dev = small.shape[0]
+        small = small.reshape(n_dev, 4 + n_experts, -1).transpose(1, 0, 2).reshape(4 + n_experts, d_model)
+        h_attn = rms_norm(tok_rows, small[0]).astype(jnp.bfloat16)
         q_proj = dot_f32(h_attn, gather_dim0(w_query)).astype(jnp.bfloat16)
         k_proj = dot_f32(h_attn, gather_dim0(w_key)).astype(jnp.bfloat16)
         v_proj = dot_f32(h_attn, gather_dim0(w_value)).astype(jnp.bfloat16)
         context_rows, k_rope, v_heads = attend_rows(q_proj, k_proj, v_proj, seq_lens)
         attn_out = dot_f32(context_rows, gather_dim0(w_attn_out))
-        mid_rows = (tok_rows.astype(jnp.float32) + rms_norm(attn_out, gather_dim0(g_attn_out))).astype(jnp.bfloat16)
-        h_moe = rms_norm(mid_rows, gather_dim0(g_moe_in)).astype(jnp.bfloat16)
-        router_probs = jax.nn.softmax(dot_f32(h_moe, gather_dim0(w_router)), axis=-1)
-        gate_probs = jnp.take_along_axis(router_probs, route_idx, axis=1)
-        moe_out = moe_rows(h_moe, gate_probs, route_idx, gather_dim1(w_gate), gather_dim1(w_up), gather_dim1(w_down))
-        y_rows = (mid_rows.astype(jnp.float32) + rms_norm(moe_out, gather_dim0(g_moe_out))).astype(jnp.bfloat16)
+        mid_rows = (tok_rows.astype(jnp.float32) + rms_norm(attn_out, small[1])).astype(jnp.bfloat16)
+        h_moe = rms_norm(mid_rows, small[2]).astype(jnp.bfloat16)
+        logits = lax.dot_general(h_moe, small[4:], (((1,), (1,)), ((), ())), preferred_element_type=jnp.float32)
+        router_probs = jax.nn.softmax(logits, axis=-1)
+        picks = (route_idx[:, :, None] == jnp.arange(n_experts)).astype(jnp.float32)
+        combine = router_probs * jnp.sum(picks, axis=1)
+
+        def inner(wg, wu):
+            gate_act = dot_f32(h_moe, wg)
+            up_act = dot_f32(h_moe, wu)
+            return (jax.nn.gelu(gate_act) * up_act).astype(jnp.bfloat16)
+
+        moe_out = None
+        groups = [(0, half, [(0, half)]), (half, n_experts, [(half, n_experts - 1), (n_experts - 1, n_experts)])]
+        for lo, hi, downs in groups:
+            wg = gather_dim1(w_gate[lo:hi])
+            wu = gather_dim1(w_up[lo:hi])
+            wd = [(a, gather_dim1(w_down[a:b])) for a, b in downs]
+            acts = [inner(wg[e - lo], wu[e - lo]) for e in range(lo, hi)]
+            for a, w_part in wd:
+                for j in range(w_part.shape[0]):
+                    e = a + j
+                    term = combine[:, e:e + 1] * dot_f32(acts[e - lo], w_part[j])
+                    moe_out = term if moe_out is None else lax.optimization_barrier(moe_out + term)
+        y_rows = (mid_rows.astype(jnp.float32) + rms_norm(moe_out, small[3])).astype(jnp.bfloat16)
         return y_rows.reshape(hidden.shape), k_rope, v_heads
 
     return jax.shard_map(

time: 2690 us -> 2500 us (0.929)
  matrix products: 498 us -> 1220 us
  local copies, waits for them, and re-layouts: 429 us -> 156 us
  Pallas kernels: 270 us -> 0 us
  other arithmetic: 403 us -> 160 us
  waiting for transfers between devices: 1010 us -> 930 us
  blocking collectives: 58.1 us -> 15.4 us
    dot_general x5 -> x28, matrix products: 327 us -> 1040 us  [dot_f32(): return jnp.dot(left_op, right_op, preferred_element_type=jnp.float32)]
    gather x8 -> x0, local copies, waits for them, and re-layouts: 313 us -> none  [the longest x2 222 us: moe_rows(): jnp.take(expert_out, jnp.argsort(pair_order), axis=0)]
    another operation x3 -> x0, Pallas kernels: 268 us -> none
    reduce_sum x2, other arithmetic: 168 us -> 0.75 us  [the longest x1 0.72 us: device_fn(): combine = router_probs * jnp.sum(picks, axis=1)]
    all_gather x3 -> x7, waiting for transfers between devices: 718 us -> 595 us  [the longest x3 318 us: device_fn(): wd = [(a, gather_dim1(w_down[a:b])) for a, b in downs]]
    all_gather x5 -> x1, blocking collectives: 58.1 us -> 15.4 us  [device_fn(): small = lax.all_gather(small, 'wg', axis=0, tiled=False)]
    slice x0 -> x7, local copies, waits for them, and re-layouts: none -> 36.2 us  [the longest x3 14 us: device_fn(): wd = [(a, gather_dim1(w_down[a:b])) for a, b in downs]]
    all_gather x1, waiting for transfers between devices: 0.01 us -> 29.3 us  [device_fn(): v_proj = dot_f32(h_attn, gather_dim0(w_value)).astype(jnp.bfloat16)]
  transfers between devices with their start and end apart: 7 -> 11, of which waited for: 4 -> 6; matrix products, arithmetic and copies ran while one was open for 34% -> 58% of each run, Pallas kernels for 6% -> 0%
where the time goes in v1:
time: 2500 us; the launch traced here: 2490 us
  matrix products  1220 us (49%)
  waiting for transfers between devices  930 us (37%)
  other arithmetic  160 us (6%)
  local copies, waits for them, and re-layouts  156 us (6%)
    dot_general x28, matrix products, dot_f32(): return jnp.dot(left_op, right_op, preferred_element_type=jnp.float32)  1040 us
    all_gather x3, waiting for transfers between devices, device_fn(): wd = [(a, gather_dim1(w_down[a:b])) for a, b in downs]  318 us
    all_gather x1, waiting for transfers between devices, device_fn(): q_proj = dot_f32(h_attn, gather_dim0(w_query)).astype(jnp.bfloat16)  301 us
    all_gather x2, waiting for transfers between devices, device_fn(): wg = gather_dim1(w_gate[lo:hi])  276 us
    dot_general x4, matrix products, attend_prompt(): jnp.einsum('kgqs,skd->qkgd', attn_probs, v_rows, preferred_element_type=j...  67.6 us
    unnamed x66, local copies, waits for them, and re-layouts  58.9 us
    dot_general x4, matrix products, attend_prompt(): jnp.einsum('qkgd,skd->kgqs', q_rows, k_rows, preferred_element_type=jnp.f...  54.5 us
  transfers between devices with their start and end apart: 11, of which 6 were waited for; matrix products, arithmetic and copies ran while one was open for 58% of the time, Pallas kernels for 0%

profile of v1, /device:TPU:0, one launch (start us, length us, event | category | flops | bytes accessed | tf_op | source)
XLA Modules:
  0.0 2491.3 jit_solution(14160097749320752105)
XLA Ops:
  47.6 15.4 all-gather
  74.1 16.6 fusion.35
  90.7 23.8 convert_bitcast_fusion.1
  118.7 29.3 %all-gather.13.cloned.1.call-done = bf16[6144,1024]{1,0:T(8,128)(2,1)} async-done(((bf16[768,1024]{1,0:T(8,128)(2,1)}), bf16[6144,1024]{1,0:T(8,128)(2,1)}) %all-gather.13.cloned.1.call-update) | async-done | bytes 12582928 | tf_op jit(solution)/shard_map/all_gather | solution.py:83
  148.1 24.5 fusion.127
  182.2 301.3 %all-gather.17.cloned.1.call-done = bf16[6144,6144]{1,0:T(8,128)(2,1)} async-done(((bf16[768,6144]{1,0:T(8,128)(2,1)}), bf16[6144,6144]{1,0:T(8,128)(2,1)}) %all-gather.17.cloned.1.call-update) | async-done | bytes 75497488 | tf_op jit(solution)/shard_map/all_gather | solution.py:81
  483.5 135.9 %convert_bitcast_fusion = f32[192,8,48,128]{3,1,2,0:T(8,128)} fusion(bf16[1536,6144]{1,0:T(8,128)(2,1)} %fusion.35, bf16[6144,6144]{1,0:T(8,128)(2,1)} %all-gather.17.cloned.1.call-done), kind=kOutput, calls=%fused_computation.44 | convolution fusion | flops 115982991360 | bytes 132120576 | tf_op jit(solution)/shard_map/dot_general | solution.py:15
  619.4 32.9 %copy.51 = f32[192,8,48,128]{3,2,1,0:T(8,128)} copy(f32[192,8,48,128]{3,1,2,0:T(8,128)} %convert_bitcast_fusion) | data formatting | bytes 75497472
  652.2 32.6 %subtract_convert_fusion = (bf16[4,384,48,64]{3,2,1,0:T(8,128)(2,1)S(1)}, bf16[4,384,48,64]{3,2,1,0:T(8,128)(2,1)}) fusion(f32[4,384,48,128]{3,2,1,0:T(8,128)} %bitcast.220, f32[384,64]{1,0:T(8,128)S(1)} %copy-done.7, f32[384,64]{1,0:T(8,128)S(1)} %copy-done.5), kind=kLoop, calls=%fused_computation.55 | loop fusion | flops 37748736 | bytes 56819712 | tf_op jit(solution)/shard_map/convert.12
  684.9 15.8 copy.39
  725.9 185.4 %while.12 = (s32[]{:T(128)}, bf16[4,384,8,6,128]{1,4,3,2,0:T(8,128)(2,1)}, bf16[4,384,8,128]{3,2,1,0:T(8,128)(2,1)}, s32[4]{0:T(128)S(1)}, bf16[4,384,8,128]{3,2...) while((s32[]{:T(128)}, bf16[4,384,8,6,128]{1,4,3,2,0:T(8,128)(2,1)}, ...), condition=%wide.region_4.5_spmd, body=%wide.region_1.4_spmd.sunk | while | flops 5516348416 | bytes 78448992 | solution.py:60
  755.5 16.9 bitcast_dynamic-update-slice_fusion.2
  801.8 16.9 bitcast_dynamic-update-slice_fusion.2
  848.1 16.9 bitcast_dynamic-update-slice_fusion.2
  894.4 16.9 bitcast_dynamic-update-slice_fusion.2
  911.3 21.7 copy.43
  943.6 138.5 %multiply_reduce_fusion.1 = (f32[1536]{0:T(1024)S(1)}, f32[1536,6144]{1,0:T(8,128)}) fusion(bf16[1536,6144]{0,1:T(8,128)(2,1)} %bitcast.225, bf16[6144,6144]{1,0:T(8,128)(2,1)} %all-gather.19.cloned.1.call-done), kind=kOutput, calls=%fused_computation.53 | convolution fusion | flops 115982991360 | bytes 132126720 | tf_op jit(solution)/shard_map/dot_general | solution.py:15
  1082.1 27.9 %fusion.29 = (f32[1536]{0:T(1024)S(1)}, bf16[1536,6144]{1,0:T(8,128)(2,1)}) fusion(f32[6144]{0:T(1024)S(1)} %bitcast.232, f32[1536,6144]{1,0:T(8,128)} %get-tuple-element.144, f32[1536]{0:T(1024)S(1)} %add_rsqrt_fusion.2, bf16[4,384,6144]{2,1,0:T(8,128)(2,1)} %param.17), kind=kLoop, calls=%fused_computation.33 | loop fusion | flops 75495936 | bytes 75534336 | tf_op jit(solution)/shard_map/reduce_sum | solution.py:20
  1133.9 26.5 %fusion.49 = f32[1536,1024]{1,0:T(8,128)} fusion(bf16[1536,6144]{1,0:T(8,128)(2,1)} %copy-done, bf16[4,6144,1024]{2,1,0:T(8,128)(2,1)} %all-gather.23.cloned.1.call-done), kind=kOutput, calls=%fused_computation.89 | convolution fusion | flops 19327352832 | bytes 37748736 | tf_op jit(solution)/shard_map/dot_general | solution.py:15
  1160.4 25.2 %fusion.52 = f32[1536,1024]{1,0:T(8,128)} fusion(bf16[1536,6144]{1,0:T(8,128)(2,1)S(1)} %copy-done.1, bf16[4,6144,1024]{2,1,0:T(8,128)(2,1)} %all-gather.23.cloned.1.call-done), kind=kOutput, calls=%fused_computation.95 | convolution fusion | flops 19327352832 | bytes 37748736 | tf_op jit(solution)/shard_map/dot_general | solution.py:15
  1185.6 89.3 %all-gather.21.cloned.1.call-done = bf16[4,6144,1024]{2,1,0:T(8,128)(2,1)} async-done(((bf16[4,768,1024]{2,1,0:T(8,128)(2,1)}), bf16[4,6144,1024]{2,1,0:T(8,128)(2,1)}) %all-gather.21.cloned.1.call-update) | async-done | bytes 50331664 | tf_op jit(solution)/shard_map/all_gather | solution.py:101
  1274.9 28.2 %fusion.72 = bf16[1536,1024]{1,0:T(8,128)(2,1)S(1)} fusion(f32[1536,1024]{1,0:T(8,128)} %fusion.49, bf16[1536,6144]{1,0:T(8,128)(2,1)} %copy-done, bf16[4,6144,1024]{2,1,0:T(8,128)(2,1)} %all-gather.21.cloned.1.call-done), kind=kOutput, calls=%fused_computation.124 | convolution fusion | flops 19343081472 | bytes 40894464 | tf_op jit(solution)/shard_map/dot_general | solution.py:15
  1303.1 28.6 %fusion.63 = bf16[1536,1024]{1,0:T(8,128)(2,1)} fusion(f32[1536,1024]{1,0:T(8,128)S(1)} %copy-done.28, bf16[1536,6144]{1,0:T(8,128)(2,1)} %copy-done, bf16[4,6144,1024]{2,1,0:T(8,128)(2,1)} %all-gather.21.cloned.1.call-done), kind=kOutput, calls=%fused_computation.115 | convolution fusion | flops 19343081472 | bytes 40894464 | tf_op jit(solution)/shard_map/dot_general | solution.py:15
  1331.7 171.4 %all-gather.25.cloned.1.call-done = bf16[4,1024,6144]{2,1,0:T(8,128)(2,1)} async-done(((bf16[4,128,6144]{2,1,0:T(8,128)(2,1)}), bf16[4,1024,6144]{2,1,0:T(8,128)(2,1)}) %all-gather.25.cloned.1.call-update) | async-done | bytes 50331664 | tf_op jit(solution)/shard_map/all_gather | solution.py:103
  1503.1 27.9 %fusion.51 = f32[1536,6144]{1,0:T(8,128)} fusion(bf16[1536,1024]{1,0:T(8,128)(2,1)} %fusion.63, bf16[4,1024,6144]{2,1,0:T(8,128)(2,1)} %all-gather.25.cloned.1.call-done), kind=kOutput, calls=%fused_computation.93 | convolution fusion | flops 19327352832 | bytes 53477376 | tf_op jit(solution)/shard_map/dot_general | solution.py:15
  1531.0 37.7 %multiply_add_fusion.6 = f32[1536,6144]{1,0:T(8,128)} fusion(f32[1536,6144]{1,0:T(8,128)} %fusion.51, bf16[1536,1024]{1,0:T(8,128)(2,1)S(1)} %fusion.72, f32[1536]{0:T(1024)S(1)} %copy-done.21, f32[1536]{0:T(1024)S(1)} %copy-done.22, bf16[4,1024,6144]{2,1,0:T(8,128)(2,1)} %all-gather.25.cloned.1.call-done), kind=kOutput, calls=%fused_computation.52 | convolution fusion | flops 19355664384 | bytes 91238400 | tf_op jit(solution)/shard_map/dot_general | solution.py:15
  1568.7 23.7 fusion.47
  1592.4 27.6 %fusion.81 = bf16[1536,1024]{1,0:T(8,128)(2,1)S(1)} fusion(f32[1536,1024]{1,0:T(8,128)S(1)} %fusion.47, bf16[1536,6144]{1,0:T(8,128)(2,1)} %copy-done, bf16[4,6144,1024]{2,1,0:T(8,128)(2,1)} %all-gather.21.cloned.1.call-done), kind=kOutput, calls=%fused_computation.133 | convolution fusion | flops 19343081472 | bytes 40894464 | tf_op jit(solution)/shard_map/dot_general | solution.py:15
  1620.0 37.4 %multiply_add_fusion.5 = f32[1536,6144]{1,0:T(8,128)} fusion(f32[1536,6144]{1,0:T(8,128)} %multiply_add_fusion.6, bf16[1536,1024]{1,0:T(8,128)(2,1)S(1)} %fusion.81, f32[1536]{0:T(1024)S(1)} %copy-done.20, bf16[4,1024,6144]{2,1,0:T(8,128)(2,1)} %all-gather.25.cloned.1.call-done), kind=kOutput, calls=%fused_computation.51 | convolution fusion | flops 19346227200 | bytes 91232256 | tf_op jit(solution)/shard_map/dot_general | solution.py:15
  1657.4 23.7 fusion.45
  1681.1 27.6 %fusion.90 = bf16[1536,1024]{1,0:T(8,128)(2,1)S(1)} fusion(f32[1536,1024]{1,0:T(8,128)S(1)} %fusion.45, bf16[1536,6144]{1,0:T(8,128)(2,1)} %copy-done, bf16[4,6144,1024]{2,1,0:T(8,128)(2,1)} %all-gather.21.cloned.1.call-done), kind=kOutput, calls=%fused_computation.142 | convolution fusion | flops 19343081472 | bytes 40894464 | tf_op jit(solution)/shard_map/dot_general | solution.py:15
  1708.7 37.5 %multiply_add_fusion.4 = f32[1536,6144]{1,0:T(8,128)} fusion(f32[1536,6144]{1,0:T(8,128)} %multiply_add_fusion.5, bf16[1536,1024]{1,0:T(8,128)(2,1)S(1)} %fusion.90, f32[1536]{0:T(1024)S(1)} %copy-done.19, bf16[4,1024,6144]{2,1,0:T(8,128)(2,1)} %all-gather.25.cloned.1.call-done), kind=kOutput, calls=%fused_computation.50 | convolution fusion | flops 19346227200 | bytes 91232256 | tf_op jit(solution)/shard_map/dot_general | solution.py:15
  1746.2 26.2 %fusion.43 = f32[1536,1024]{1,0:T(8,128)} fusion(bf16[1536,6144]{1,0:T(8,128)(2,1)} %copy-done, bf16[4,6144,1024]{2,1,0:T(8,128)(2,1)} %all-gather.29.cloned.1.call-done), kind=kOutput, calls=%fused_computation.74 | convolution fusion | flops 19327352832 | bytes 37748736 | tf_op jit(solution)/shard_map/dot_general | solution.py:15
  1772.4 187.2 %all-gather.27.cloned.1.call-done = bf16[4,6144,1024]{2,1,0:T(8,128)(2,1)} async-done(((bf16[4,768,1024]{2,1,0:T(8,128)(2,1)}), bf16[4,6144,1024]{2,1,0:T(8,128)(2,1)}) %all-gather.27.cloned.1.call-update) | async-done | bytes 50331664 | tf_op jit(solution)/shard_map/all_gather | solution.py:101
  1959.6 28.0 %fusion.99 = bf16[1536,1024]{1,0:T(8,128)(2,1)S(1)} fusion(f32[1536,1024]{1,0:T(8,128)} %fusion.43, bf16[1536,6144]{1,0:T(8,128)(2,1)} %copy-done, bf16[4,6144,1024]{2,1,0:T(8,128)(2,1)} %all-gather.27.cloned.1.call-done), kind=kOutput, calls=%fused_computation.151 | convolution fusion | flops 19343081472 | bytes 40894464 | tf_op jit(solution)/shard_map/dot_general | solution.py:15
  1987.6 147.0 %all-gather.31.cloned.1.call-done = bf16[3,1024,6144]{2,1,0:T(8,128)(2,1)} async-done(((bf16[3,128,6144]{2,1,0:T(8,128)(2,1)}), bf16[3,1024,6144]{2,1,0:T(8,128)(2,1)}) %all-gather.31.cloned.1.call-update) | async-done | bytes 37748752 | tf_op jit(solution)/shard_map/all_gather | solution.py:103
  2134.6 37.7 %multiply_add_fusion.3 = f32[1536,6144]{1,0:T(8,128)} fusion(f32[1536,6144]{1,0:T(8,128)} %multiply_add_fusion.4, bf16[1536,1024]{1,0:T(8,128)(2,1)S(1)} %fusion.99, f32[1536]{0:T(1024)S(1)} %copy-done.18, bf16[3,1024,6144]{2,1,0:T(8,128)(2,1)} %all-gather.31.cloned.1.call-done), kind=kOutput, calls=%fused_computation.49 | convolution fusion | flops 19346227200 | bytes 91232256 | tf_op jit(solution)/shard_map/dot_general | solution.py:15
  2172.2 26.5 %fusion.39 = f32[1536,1024]{1,0:T(8,128)} fusion(bf16[1536,6144]{1,0:T(8,128)(2,1)} %copy-done, bf16[4,6144,1024]{2,1,0:T(8,128)(2,1)} %all-gather.29.cloned.1.call-done), kind=kOutput, calls=%fused_computation.64 | convolution fusion | flops 19327352832 | bytes 37748736 | tf_op jit(solution)/shard_map/dot_general | solution.py:15
  2198.7 28.5 %fusion.41 = f32[1536,1024]{1,0:T(8,128)S(1)} fusion(bf16[1536,6144]{1,0:T(8,128)(2,1)S(1)} %copy-done.2, bf16[4,6144,1024]{2,1,0:T(8,128)(2,1)} %all-gather.29.cloned.1.call-done), kind=kOutput, calls=%fused_computation.69 | convolution fusion | flops 19327352832 | bytes 37748736 | tf_op jit(solution)/shard_map/dot_general | solution.py:15
  2227.2 27.8 %fusion.108 = bf16[1536,1024]{1,0:T(8,128)(2,1)S(1)} fusion(f32[1536,1024]{1,0:T(8,128)S(1)} %fusion.41, bf16[1536,6144]{1,0:T(8,128)(2,1)} %copy-done, bf16[4,6144,1024]{2,1,0:T(8,128)(2,1)} %all-gather.27.cloned.1.call-done), kind=kOutput, calls=%fused_computation.160 | convolution fusion | flops 19343081472 | bytes 40894464 | tf_op jit(solution)/shard_map/dot_general | solution.py:15
  2255.0 37.3 %multiply_add_fusion.2 = f32[1536,6144]{1,0:T(8,128)} fusion(f32[1536,6144]{1,0:T(8,128)} %multiply_add_fusion.3, bf16[1536,1024]{1,0:T(8,128)(2,1)S(1)} %fusion.108, f32[1536]{0:T(1024)S(1)} %copy-done.17, bf16[3,1024,6144]{2,1,0:T(8,128)(2,1)} %all-gather.31.cloned.1.call-done), kind=kOutput, calls=%fused_computation.48 | convolution fusion | flops 19346227200 | bytes 91232256 | tf_op jit(solution)/shard_map/dot_general | solution.py:15
  2292.3 28.0 %fusion.117 = bf16[1536,1024]{1,0:T(8,128)(2,1)S(1)} fusion(f32[1536,1024]{1,0:T(8,128)} %fusion.39, bf16[1536,6144]{1,0:T(8,128)(2,1)} %copy-done, bf16[4,6144,1024]{2,1,0:T(8,128)(2,1)} %all-gather.27.cloned.1.call-done), kind=kOutput, calls=%fused_computation.169 | convolution fusion | flops 19343081472 | bytes 40894464 | tf_op jit(solution)/shard_map/dot_general | solution.py:15
  2320.4 37.7 %multiply_add_fusion.1 = f32[1536,6144]{1,0:T(8,128)} fusion(f32[1536,6144]{1,0:T(8,128)} %multiply_add_fusion.2, bf16[1536,1024]{1,0:T(8,128)(2,1)S(1)} %fusion.117, f32[1536]{0:T(1024)S(1)} %copy-done.16, bf16[3,1024,6144]{2,1,0:T(8,128)(2,1)} %all-gather.31.cloned.1.call-done), kind=kOutput, calls=%fused_computation.47 | convolution fusion | flops 19346227200 | bytes 91232256 | tf_op jit(solution)/shard_map/dot_general | solution.py:15
  2358.0 23.7 fusion.37
  2381.7 27.6 %fusion.126 = bf16[1536,1024]{1,0:T(8,128)(2,1)S(1)} fusion(f32[1536,1024]{1,0:T(8,128)S(1)} %fusion.37, bf16[1536,6144]{1,0:T(8,128)(2,1)} %copy-done, bf16[4,6144,1024]{2,1,0:T(8,128)(2,1)} %all-gather.27.cloned.1.call-done), kind=kOutput, calls=%fused_computation.178 | convolution fusion | flops 19343081472 | bytes 40894464 | tf_op jit(solution)/shard_map/dot_general | solution.py:15
  2409.3 36.0 %multiply_add_fusion = f32[1536,6144]{1,0:T(8,128)} fusion(f32[1536,6144]{1,0:T(8,128)} %multiply_add_fusion.1, bf16[1536,1024]{1,0:T(8,128)(2,1)S(1)} %fusion.126, f32[1536]{0:T(1024)S(1)} %copy-done.15, bf16[1,1024,6144]{2,1,0:T(8,128)(2,1)} %all-gather.33.cloned.1.call-done), kind=kOutput, calls=%fused_computation.46 | convolution fusion | flops 19346227200 | bytes 91232256 | tf_op jit(solution)/shard_map/dot_general | solution.py:15
  2445.3 13.6 multiply_reduce_fusion
  2459.0 25.6 %fusion.32 = bf16[1536,6144]{1,0:T(8,128)(2,1)} fusion(bf16[1536,6144]{1,0:T(8,128)(2,1)} %get-tuple-element.126, f32[1536,6144]{1,0:T(8,128)} %multiply_add_fusion, f32[6144]{0:T(1024)S(1)} %bitcast.231, f32[1536]{0:T(1024)S(1)} %add_rsqrt_fusion), kind=kLoop, calls=%fused_computation.36 | loop fusion | flops 47185920 | bytes 75528192 | tf_op jit(solution)/shard_map/convert_element_type | solution.py:110
  (150 shorter events, 242.3 us)
Async XLA Ops:
  7.2 83.6 %all-gather.15.cloned.1.call-start = ((), (), s32[]{:S(2)}) async-start(), calls=%async_computation.1 | async-start | bytes 14155776 | tf_op jit(solution)/shard_map/all_gather | solution.py:82
  7.9 140.2 %all-gather.13.cloned.1.call-start = ((), (), s32[]{:S(2)}) async-start(), calls=%async_computation | async-start | bytes 14155776 | tf_op jit(solution)/shard_map/all_gather | solution.py:83
  8.6 474.8 %all-gather.17.cloned.1.call-start = ((), (), s32[]{:S(2)}) async-start(), calls=%async_computation.2 | async-start | bytes 84934656 | tf_op jit(solution)/shard_map/all_gather | solution.py:81
  9.4 934.2 %all-gather.19.cloned.1.call-start = ((), (), s32[]{:S(2)}) async-start(), calls=%async_computation.3 | async-start | bytes 84934656 | tf_op jit(solution)/shard_map/all_gather | solution.py:85
  10.0 1123.9 %all-gather.23.cloned.1.call-start = ((), (), s32[]{:S(2)}) async-start(), calls=%async_computation.5 | async-start | bytes 56623104 | tf_op jit(solution)/shard_map/all_gather | solution.py:102
  20.5 1254.4 %all-gather.21.cloned.1.call-start = ((), (), s32[]{:S(2)}) async-start(), calls=%async_computation.4 | async-start | bytes 56623104 | tf_op jit(solution)/shard_map/all_gather | solution.py:101
  30.9 1472.2 %all-gather.25.cloned.1.call-start = ((), (), s32[]{:S(2)}) async-start(), calls=%async_computation.6 | async-start | bytes 56623104 | tf_op jit(solution)/shard_map/all_gather | solution.py:103
  37.2 1708.9 %all-gather.29.cloned.1.call-start = ((), (), s32[]{:S(2)}) async-start(), calls=%async_computation.8 | async-start | bytes 56623104 | tf_op jit(solution)/shard_map/all_gather | solution.py:102
  38.0 1921.6 %all-gather.27.cloned.1.call-start = ((), (), s32[]{:S(2)}) async-start(), calls=%async_computation.7 | async-start | bytes 56623104 | tf_op jit(solution)/shard_map/all_gather | solution.py:101
  38.0 8.6 copy-start.13
  38.1 8.7 copy-start.23
  38.1 8.9 copy-start.24
  38.1 9.1 copy-start.25
  38.1 9.3 copy-start.26
  38.7 2095.8 %all-gather.31.cloned.1.call-start = ((), (), s32[]{:S(2)}) async-start(), calls=%async_computation.9 | async-start | bytes 42467328 | tf_op jit(solution)/shard_map/all_gather | solution.py:103
  43.9 29.5 %copy-start.14 = (s32[1536,2]{0,1:T(2,128)S(1)}, s32[1536,2]{0,1:T(2,128)}, u32[]{:S(2)}) copy-start(s32[1536,2]{0,1:T(2,128)} %param.19) | copy-start | bytes 36868
  43.9 2365.5 %all-gather.33.cloned.1.call-start = ((), (), s32[]{:S(2)}) async-start(), calls=%async_computation.10 | async-start | bytes 14155776 | tf_op jit(solution)/shard_map/all_gather | solution.py:103
  73.3 101.7 %copy-start.4 = (f32[384,64]{1,0:T(8,128)}, f32[384,64]{1,0:T(8,128)S(1)}, u32[]{:S(2)}) copy-start(f32[384,64]{1,0:T(8,128)S(1)} %get-tuple-element.141) | copy-start | bytes 294916
  73.4 101.7 %copy-start.6 = (f32[384,64]{1,0:T(8,128)}, f32[384,64]{1,0:T(8,128)S(1)}, u32[]{:S(2)}) copy-start(f32[384,64]{1,0:T(8,128)S(1)} %get-tuple-element.142) | copy-start | bytes 294916
  172.5 3.9 copy-start.3
  619.4 32.9 %copy-start.5 = (f32[384,64]{1,0:T(8,128)S(1)}, f32[384,64]{1,0:T(8,128)}, u32[]{:S(2)}) copy-start(f32[384,64]{1,0:T(8,128)} %copy-done.4) | copy-start | bytes 294916
  619.4 32.9 %copy-start.7 = (f32[384,64]{1,0:T(8,128)S(1)}, f32[384,64]{1,0:T(8,128)}, u32[]{:S(2)}) copy-start(f32[384,64]{1,0:T(8,128)} %copy-done.6) | copy-start | bytes 294916
  713.1 12.8 copy-start.27
  943.6 138.5 %copy-start.11 = (f32[1,8,768]{2,0,1:T(1,128)S(1)}, f32[1,8,768]{2,0,1:T(1,128)}, u32[]{:S(2)}) copy-start(f32[1,8,768]{2,0,1:T(1,128)} %get-tuple-element.139) | copy-start | bytes 73732
  1082.1 27.9 %copy-start.12 = (f32[1,8,768]{2,0,1:T(1,128)S(1)}, f32[1,8,768]{2,0,1:T(1,128)}, u32[]{:S(2)}) copy-start(f32[1,8,768]{2,0,1:T(1,128)} %get-tuple-element.138) | copy-start | bytes 73732
  1110.0 18.1 copy-start.8
  1121.7 6.4 copy-start
  1121.8 11.4 copy-start.9
  1133.9 26.5 %copy-start.1 = (bf16[1536,6144]{1,0:T(8,128)(2,1)S(1)}, bf16[1536,6144]{1,0:T(8,128)(2,1)}, u32[]{:S(2)}) copy-start(bf16[1536,6144]{1,0:T(8,128)(2,1)} %copy-done) | copy-start | bytes 56623108
  1274.9 28.2 %copy-start.28 = (f32[1536,1024]{1,0:T(8,128)S(1)}, f32[1536,1024]{1,0:T(8,128)}, u32[]{:S(2)}) copy-start(f32[1536,1024]{1,0:T(8,128)} %fusion.52) | copy-start | bytes 18874372
  1331.7 199.3 %copy-start.21 = (f32[1536]{0:T(1024)S(1)}, f32[1536]{0:T(1024)}, u32[]{:S(2)}) copy-start(f32[1536]{0:T(1024)} %get-tuple-element.111) | copy-start | bytes 18436
  1331.7 199.3 %copy-start.22 = (f32[1536]{0:T(1024)S(1)}, f32[1536]{0:T(1024)}, u32[]{:S(2)}) copy-start(f32[1536]{0:T(1024)} %get-tuple-element.112) | copy-start | bytes 18436
  1592.4 27.6 %copy-start.20 = (f32[1536]{0:T(1024)S(1)}, f32[1536]{0:T(1024)}, u32[]{:S(2)}) copy-start(f32[1536]{0:T(1024)} %get-tuple-element.110) | copy-start | bytes 18436
  1681.1 27.6 %copy-start.19 = (f32[1536]{0:T(1024)S(1)}, f32[1536]{0:T(1024)}, u32[]{:S(2)}) copy-start(f32[1536]{0:T(1024)} %get-tuple-element.109) | copy-start | bytes 18436
  1772.4 362.1 %copy-start.18 = (f32[1536]{0:T(1024)S(1)}, f32[1536]{0:T(1024)}, u32[]{:S(2)}) copy-start(f32[1536]{0:T(1024)} %get-tuple-element.108) | copy-start | bytes 18436
  2172.2 26.5 %copy-start.2 = (bf16[1536,6144]{1,0:T(8,128)(2,1)S(1)}, bf16[1536,6144]{1,0:T(8,128)(2,1)}, u32[]{:S(2)}) copy-start(bf16[1536,6144]{1,0:T(8,128)(2,1)} %copy-done) | copy-start | bytes 56623108
  2227.2 27.8 %copy-start.17 = (f32[1536]{0:T(1024)S(1)}, f32[1536]{0:T(1024)}, u32[]{:S(2)}) copy-start(f32[1536]{0:T(1024)} %get-tuple-element.107) | copy-start | bytes 18436
  2292.3 28.1 %copy-start.16 = (f32[1536]{0:T(1024)S(1)}, f32[1536]{0:T(1024)}, u32[]{:S(2)}) copy-start(f32[1536]{0:T(1024)} %get-tuple-element.106) | copy-start | bytes 18436
  2381.7 27.6 %copy-start.15 = (f32[1536]{0:T(1024)S(1)}, f32[1536]{0:T(1024)}, u32[]{:S(2)}) copy-start(f32[1536]{0:T(1024)} %get-tuple-element.105) | copy-start | bytes 18436
  2445.3 13.7 copy-start.10
Sparse Core Ops, SparseCore 0:
  9.8 70.0 all-gather.14
  81.7 66.2 all-gather.12
  149.9 333.5 all-gather.16
  485.2 333.5 all-gather.18
  820.5 226.3 all-gather.22
  1048.5 226.3 all-gather.20
  1276.8 226.3 all-gather.24
  1505.0 226.3 all-gather.28
  1733.2 226.3 all-gather.26
  1961.3 173.2 all-gather.30
  2136.4 66.2 all-gather.32

commit v2 on v1

--- a/solution.py
+++ b/solution.py
@@ -2,6 +2,8 @@
 import jax
 import jax.numpy as jnp
 from jax import lax
+from jax.experimental import pallas as pl
+from jax.experimental.pallas import tpu as pltpu
 from jax.sharding import PartitionSpec as P
 
 HEAD_DIM = 128
@@ -61,6 +63,90 @@
     return context.reshape(n_prompts * seq_len, n_heads * HEAD_DIM), k_rope, v_heads
 
 
+def group_down_kernel(n_act, has_acc, *refs):
+    act_refs = refs[:n_act]
+    weight_ref, comb_ref = refs[n_act:n_act + 2]
+    acc_ref = refs[n_act + 2] if has_acc else None
+    out_ref = refs[-1]
+    block = 512
+
+    @pl.loop(0, out_ref.shape[0] // block)
+    def _(m):
+        rows = pl.ds(pl.multiple_of(m * block, block), block)
+        total = acc_ref[rows, :] if has_acc else None
+        for i in range(n_act):
+            term = comb_ref[rows, i:i + 1] * dot_f32(act_refs[i][rows, :], weight_ref[i])
+            total = term if total is None else total + term
+        out_ref[rows, :] = total
+
+
+def group_down(acts, weights, comb, acc):
+    n_act = len(acts)
+    rows, ff = acts[0].shape
+    d_model = weights.shape[2]
+    block = 512
+    col_map = lambda n: (0, n)
+    whole_map = lambda n: (0, 0)
+    in_specs = [pl.BlockSpec((rows, ff), whole_map, pipeline_mode=pl.Buffered(1)) for _ in acts]
+    in_specs.append(pl.BlockSpec((n_act, ff, block), lambda n: (0, 0, n)))
+    in_specs.append(pl.BlockSpec((rows, n_act), whole_map))
+    operands = [*acts, weights, comb]
+    if acc is not None:
+        in_specs.append(pl.BlockSpec((rows, block), col_map))
+        operands.append(acc)
+    return pl.pallas_call(
+        functools.partial(group_down_kernel, n_act, acc is not None),
+        grid=(d_model // block,),
+        in_specs=in_specs,
+        out_specs=pl.BlockSpec((rows, block), col_map),
+        out_shape=jax.ShapeDtypeStruct((rows, d_model), jnp.float32),
+        compiler_params=pltpu.CompilerParams(vmem_limit_bytes=60 * 1024 * 1024),
+        cost_estimate=pl.CostEstimate(flops=2 * n_act * rows * ff * d_model, bytes_accessed=rows * d_model * 8, transcendentals=0),
+        name='group_down',
+    )(*operands)
+
+
+def last_down_kernel(act_ref, weight_ref, comb_ref, acc_ref, mid_ref, gain_ref, out_ref, sum_ref):
+    d_model = out_ref.shape[1]
+    step = d_model // 6
+    square_sum = jnp.zeros((out_ref.shape[0], 1), jnp.float32)
+    for j in range(6):
+        cols = slice(j * step, (j + 1) * step)
+        part = acc_ref[:, cols] + comb_ref[...] * dot_f32(act_ref[...], weight_ref[:, cols])
+        sum_ref[:, cols] = part
+        square_sum += jnp.sum(part * part, axis=-1, keepdims=True)
+    inv_rms = lax.rsqrt(square_sum * (1.0 / d_model) + NORM_EPS)
+    for j in range(6):
+        cols = slice(j * step, (j + 1) * step)
+        out_ref[:, cols] = (mid_ref[:, cols].astype(jnp.float32) + sum_ref[:, cols] * inv_rms * gain_ref[:, cols]).astype(jnp.bfloat16)
+
+
+def last_down(act, weight, comb, acc, mid, gain):
+    rows, ff = act.shape
+    d_model = weight.shape[1]
+    block = 256
+    row_map = lambda m: (m, 0)
+    whole_map = lambda m: (0, 0)
+    return pl.pallas_call(
+        last_down_kernel,
+        grid=(rows // block,),
+        in_specs=[
+            pl.BlockSpec((block, ff), row_map),
+            pl.BlockSpec((ff, d_model), whole_map, pipeline_mode=pl.Buffered(1)),
+            pl.BlockSpec((block, 1), row_map),
+            pl.BlockSpec((block, d_model), row_map),
+            pl.BlockSpec((block, d_model), row_map),
+            pl.BlockSpec((1, d_model), whole_map),
+        ],
+        out_specs=pl.BlockSpec((block, d_model), row_map),
+        out_shape=jax.ShapeDtypeStruct((rows, d_model), jnp.bfloat16),
+        scratch_shapes=[pltpu.VMEM((block, d_model), jnp.float32)],
+        compiler_params=pltpu.CompilerParams(vmem_limit_bytes=60 * 1024 * 1024),
+        cost_estimate=pl.CostEstimate(flops=2 * rows * ff * d_model, bytes_accessed=rows * d_model * 8, transcendentals=0),
+        name='last_down',
+    )(act, weight, comb, acc, mid, gain)
+
+
 def solution(mesh):
     row_spec = P(('dp', 'wg'))
     dim0_spec = P('wg', None)
@@ -70,8 +156,8 @@
 
     def device_fn(hidden, seq_lens, route_idx, g_attn_in, w_query, w_key, w_value, w_attn_out, g_attn_out, g_moe_in, w_router, w_gate, w_up, w_down, g_moe_out):
         n_prompts, seq_len, d_model = hidden.shape
-        n_experts = w_gate.shape[0]
-        half = n_experts // 2
+        n_experts, local_rows, ff_dim = w_gate.shape
+        kv_dim = w_key.shape[1]
         tok_rows = hidden.reshape(n_prompts * seq_len, d_model)
         small = jnp.concatenate([g_attn_in, g_attn_out, g_moe_in, g_moe_out, w_router.T.reshape(-1)])
         small = lax.all_gather(small, 'wg', axis=0, tiled=False)
@@ -79,8 +165,9 @@
         small = small.reshape(n_dev, 4 + n_experts, -1).transpose(1, 0, 2).reshape(4 + n_experts, d_model)
         h_attn = rms_norm(tok_rows, small[0]).astype(jnp.bfloat16)
         q_proj = dot_f32(h_attn, gather_dim0(w_query)).astype(jnp.bfloat16)
-        k_proj = dot_f32(h_attn, gather_dim0(w_key)).astype(jnp.bfloat16)
-        v_proj = dot_f32(h_attn, gather_dim0(w_value)).astype(jnp.bfloat16)
+        q_proj, h_attn = lax.optimization_barrier((q_proj, h_attn))
+        kv_proj = dot_f32(h_attn, gather_dim0(jnp.concatenate([w_key, w_value], axis=1))).astype(jnp.bfloat16)
+        k_proj, v_proj = kv_proj[:, :kv_dim], kv_proj[:, kv_dim:]
         context_rows, k_rope, v_heads = attend_rows(q_proj, k_proj, v_proj, seq_lens)
         attn_out = dot_f32(context_rows, gather_dim0(w_attn_out))
         mid_rows = (tok_rows.astype(jnp.float32) + rms_norm(attn_out, small[1])).astype(jnp.bfloat16)
@@ -90,24 +177,25 @@
         picks = (route_idx[:, :, None] == jnp.arange(n_experts)).astype(jnp.float32)
         combine = router_probs * jnp.sum(picks, axis=1)
 
-        def inner(wg, wu):
-            gate_act = dot_f32(h_moe, wg)
-            up_act = dot_f32(h_moe, wu)
+        def inner(h_in, w_gate_e, w_up_e):
+            gate_act = dot_f32(h_in, w_gate_e)
+            up_act = dot_f32(h_in, w_up_e)
             return (jax.nn.gelu(gate_act) * up_act).astype(jnp.bfloat16)
 
-        moe_out = None
-        groups = [(0, half, [(0, half)]), (half, n_experts, [(half, n_experts - 1), (n_experts - 1, n_experts)])]
-        for lo, hi, downs in groups:
-            wg = gather_dim1(w_gate[lo:hi])
-            wu = gather_dim1(w_up[lo:hi])
-            wd = [(a, gather_dim1(w_down[a:b])) for a, b in downs]
-            acts = [inner(wg[e - lo], wu[e - lo]) for e in range(lo, hi)]
-            for a, w_part in wd:
-                for j in range(w_part.shape[0]):
-                    e = a + j
-                    term = combine[:, e:e + 1] * dot_f32(acts[e - lo], w_part[j])
-                    moe_out = term if moe_out is None else lax.optimization_barrier(moe_out + term)
-        y_rows = (mid_rows.astype(jnp.float32) + rms_norm(moe_out, small[3])).astype(jnp.bfloat16)
+        acts = []
+        for lo, hi in ((0, 4), (4, 8)):
+            n_part = hi - lo
+            packed = gather_dim1(jnp.concatenate([w_gate[lo:hi], w_up[lo:hi]], axis=0))
+            for i in range(n_part):
+                act = inner(h_moe, packed[i], packed[n_part + i])
+                act, h_moe = lax.optimization_barrier((act, h_moe))
+                acts.append(act)
+        *acts, = lax.optimization_barrier(tuple(acts))
+        moe_acc = None
+        for lo, hi in ((0, 4), (4, 7)):
+            moe_acc = group_down(acts[lo:hi], gather_dim1(w_down[lo:hi]), combine[:, lo:hi], moe_acc)
+        act_7, down_7 = acts[7], gather_dim1(w_down[7:8])[0]
+        y_rows = last_down(act_7, down_7, combine[:, 7:8], moe_acc, mid_rows, small[3].astype(jnp.float32)[None])
         return y_rows.reshape(hidden.shape), k_rope, v_heads
 
     return jax.shard_map(

time: 2500 us -> 2220 us (0.89)
  matrix products: 1220 us -> 916 us
  Pallas kernels: 0 us -> 207 us
  waiting for transfers between devices: 930 us -> 742 us
    dot_general x28 -> x19, matrix products: 1040 us -> 739 us  [dot_f32(): return jnp.dot(left_op, right_op, preferred_element_type=jnp.float32)]
    pallas_call x0 -> x3, Pallas kernels: none -> 207 us  [the longest x2 165 us: group_down(): pl.pallas_call(functools.partial(group_down_kernel, n_act, acc is not Non...]
    all_gather x9 -> x6, waiting for transfers between devices: 624 us -> 497 us  [the longest x2 395 us: device_fn(): packed = gather_dim1(jnp.concatenate([w_gate[lo:hi], w_up[lo:hi]], axis=0))]
    all_gather x1, waiting for transfers between devices: 301 us -> 244 us  [device_fn(): q_proj = dot_f32(h_attn, gather_dim0(w_query)).astype(jnp.bfloat16)]
    convert_element_type x2 -> x1, other arithmetic: 26.3 us -> 0.64 us  [device_fn(): small[3].astype(jnp.float32)[None]]
    unnamed x66 -> x40, local copies, waits for them, and re-layouts: 58.9 us -> 41.2 us
  transfers between devices with their start and end apart: 11 -> 8, of which waited for: 6 -> 5; matrix products, arithmetic and copies ran while one was open for 58% -> 55% of each run, Pallas kernels for 0% -> 7%
where the time goes in v2:
time: 2220 us; the launch traced here: 2210 us
  matrix products  916 us (41%)
  waiting for transfers between devices  742 us (33%)
  Pallas kernels  207 us (9%)
  other arithmetic  177 us (8%)
  local copies, waits for them, and re-layouts  139 us (6%)
    dot_general x19, matrix products, dot_f32(): return jnp.dot(left_op, right_op, preferred_element_type=jnp.float32)  739 us
    all_gather x2, waiting for transfers between devices, device_fn(): packed = gather_dim1(jnp.concatenate([w_gate[lo:hi], w_up[lo:hi]], axis=0))  395 us
    all_gather x1, waiting for transfers between devices, device_fn(): q_proj = dot_f32(h_attn, gather_dim0(w_query)).astype(jnp.bfloat16)  244 us
    pallas_call x2, Pallas kernels, group_down(): pl.pallas_call(functools.partial(group_down_kernel, n_act, acc is not Non...  165 us
    all_gather x2, waiting for transfers between devices, device_fn(): gather_dim1(w_down[lo:hi])  102 us
    dot_general x4, matrix products, attend_prompt(): jnp.einsum('kgqs,skd->qkgd', attn_probs, v_rows, preferred_element_type=j...  68.3 us
    dot_general x4, matrix products, attend_prompt(): jnp.einsum('qkgd,skd->kgqs', q_rows, k_rows, preferred_element_type=jnp.f...  54.4 us
    sub x4, matrix products, attend_prompt(): attn_probs = jax.nn.softmax(scores, axis=-1).astype(jnp.bfloat16)  50 us
  transfers between devices with their start and end apart: 8, of which 5 were waited for; matrix products, arithmetic and copies ran while one was open for 55% of the time, Pallas kernels for 7%

profile of v2, /device:TPU:0, one launch (start us, length us, event | category | flops | bytes accessed | tf_op | source)
XLA Modules:
  0.0 2212.3 jit_solution(16570656913722391574)
XLA Ops:
  12.7 14.4 fusion.131
  58.1 15.3 all-gather
  86.3 16.7 fusion.34
  103.0 244.2 %all-gather.10.cloned.1.call-done = bf16[6144,6144]{1,0:T(8,128)(2,1)} async-done(((bf16[768,6144]{1,0:T(8,128)(2,1)}), bf16[6144,6144]{1,0:T(8,128)(2,1)}) %all-gather.10.cloned.1.call-update) | async-done | bytes 75497488 | tf_op jit(solution)/shard_map/all_gather | solution.py:167
  347.2 133.7 %convolution_convert_fusion = bf16[1536,6144]{1,0:T(8,128)(2,1)} fusion(bf16[1536,6144]{1,0:T(8,128)(2,1)} %fusion.34, bf16[6144,6144]{1,0:T(8,128)(2,1)} %all-gather.10.cloned.1.call-done), kind=kOutput, calls=%fused_computation.46 | convolution fusion | flops 115973554176 | bytes 113246208 | tf_op jit(solution)/shard_map/dot_general | solution.py:17
  480.9 48.3 %convolution_convert_fusion.1 = bf16[1536,2048]{1,0:T(8,128)(2,1)} fusion(bf16[1536,6144]{1,0:T(8,128)(2,1)} %fusion.34, bf16[6144,2048]{1,0:T(8,128)(2,1)} %all-gather.12.cloned.1.call-done), kind=kOutput, calls=%fused_computation.90 | convolution fusion | flops 38657851392 | bytes 50331648 | tf_op jit(solution)/shard_map/dot_general | solution.py:17
  550.4 16.1 copy.65
  572.8 39.3 %subtract_convert_fusion = (bf16[4,384,48,64]{3,2,1,0:T(8,128)(2,1)}, bf16[4,384,48,64]{3,2,1,0:T(8,128)(2,1)}) fusion(f32[4,384,48,128]{3,2,1,0:T(8,128)} %bitcast.189, f32[384,64]{1,0:T(8,128)S(1)} %copy-done.5, f32[384,64]{1,0:T(8,128)S(1)} %copy-done.4), kind=kLoop, calls=%fused_computation.45 | loop fusion | flops 37748736 | bytes 56819712 | tf_op jit(solution)/shard_map/convert.12
  624.6 20.3 copy.51
  650.8 20.3 pad_maximum_fusion
  671.1 186.3 %while.12 = (s32[]{:T(128)}, bf16[4,384,8,6,128]{1,4,3,2,0:T(8,128)(2,1)}, bf16[4,384,8,128]{3,2,1,0:T(8,128)(2,1)}, s32[4]{0:T(128)S(1)}, bf16[4,384,8,128]{3,2...) while((s32[]{:T(128)}, bf16[4,384,8,6,128]{1,4,3,2,0:T(8,128)(2,1)}, ...), condition=%wide.region_4.5_spmd, body=%wide.region_1.4_spmd.sunk | while | flops 5516348416 | bytes 78448992 | solution.py:62
  674.1 12.5 fusion.169
  686.6 13.6 fusion.170
  700.8 17.1 bitcast_dynamic-update-slice_fusion.2
  720.7 12.5 fusion.169
  733.2 13.6 fusion.170
  747.3 17.1 bitcast_dynamic-update-slice_fusion.2
  767.2 12.5 fusion.169
  779.7 13.6 fusion.170
  793.9 17.1 bitcast_dynamic-update-slice_fusion.2
  826.2 13.6 fusion.170
  840.4 17.1 bitcast_dynamic-update-slice_fusion.2
  857.5 21.7 copy.54
  889.8 138.5 %multiply_reduce_fusion = (f32[1536]{0:T(1024)S(1)}, f32[1536,6144]{1,0:T(8,128)}) fusion(bf16[1536,6144]{0,1:T(8,128)(2,1)} %bitcast.195, bf16[6144,6144]{1,0:T(8,128)(2,1)} %all-gather.14.cloned.1.call-done), kind=kOutput, calls=%fused_computation.43 | convolution fusion | flops 115982991360 | bytes 132126720 | tf_op jit(solution)/shard_map/dot_general | solution.py:17
  1028.3 28.0 %fusion.29 = (f32[1536]{0:T(1024)S(1)}, bf16[1536,6144]{1,0:T(8,128)(2,1)}) fusion(f32[6144]{0:T(1024)S(1)} %bitcast.202, f32[1536,6144]{1,0:T(8,128)} %get-tuple-element.194, f32[1536]{0:T(1024)S(1)} %add_rsqrt_fusion.1, bf16[4,384,6144]{2,1,0:T(8,128)(2,1)} %param.17), kind=kLoop, calls=%fused_computation.32 | loop fusion | flops 75495936 | bytes 75534336 | tf_op jit(solution)/shard_map/reduce_sum | solution.py:22
  1083.4 162.7 %all-gather.16.cloned.1.call-done = bf16[8,6144,1024]{2,1,0:T(8,128)(2,1)} async-done(((bf16[8,768,1024]{2,1,0:T(8,128)(2,1)}), bf16[8,6144,1024]{2,1,0:T(8,128)(2,1)}) %all-gather.16.cloned.1.call-update) | async-done | bytes 100663312 | tf_op jit(solution)/shard_map/all_gather | solution.py:188
  1246.1 23.7 %fusion.50 = f32[1536,1024]{1,0:T(8,128)S(1)} fusion(bf16[1536,6144]{1,0:T(8,128)(2,1)} %copy-done, bf16[8,6144,1024]{2,1,0:T(8,128)(2,1)} %all-gather.16.cloned.1.call-done), kind=kOutput, calls=%fused_computation.77 | convolution fusion | flops 19327352832 | bytes 37748736 | tf_op jit(solution)/shard_map/dot_general | solution.py:17
  1269.8 28.6 %fusion.60.refs_0_ = bf16[1536,1024]{1,0:T(8,128)(2,1)} fusion(f32[1536,1024]{1,0:T(8,128)S(1)} %fusion.50, bf16[1536,6144]{1,0:T(8,128)(2,1)} %copy-done, bf16[8,6144,1024]{2,1,0:T(8,128)(2,1)} %all-gather.16.cloned.1.call-done), kind=kOutput, calls=%fused_computation.99 | convolution fusion | flops 19343081472 | bytes 40894464 | tf_op jit(solution)/shard_map/dot_general | solution.py:17
  1298.5 23.7 %fusion.48 = f32[1536,1024]{1,0:T(8,128)S(1)} fusion(bf16[1536,6144]{1,0:T(8,128)(2,1)} %copy-done, bf16[8,6144,1024]{2,1,0:T(8,128)(2,1)} %all-gather.16.cloned.1.call-done), kind=kOutput, calls=%fused_computation.73 | convolution fusion | flops 19327352832 | bytes 37748736 | tf_op jit(solution)/shard_map/dot_general | solution.py:17
  1322.2 28.5 %fusion.69.refs_1_ = bf16[1536,1024]{1,0:T(8,128)(2,1)} fusion(f32[1536,1024]{1,0:T(8,128)S(1)} %fusion.48, bf16[1536,6144]{1,0:T(8,128)(2,1)} %copy-done, bf16[8,6144,1024]{2,1,0:T(8,128)(2,1)} %all-gather.16.cloned.1.call-done), kind=kOutput, calls=%fused_computation.108 | convolution fusion | flops 19343081472 | bytes 40894464 | tf_op jit(solution)/shard_map/dot_general | solution.py:17
  1350.7 23.9 %fusion.46 = f32[1536,1024]{1,0:T(8,128)S(1)} fusion(bf16[1536,6144]{1,0:T(8,128)(2,1)} %copy-done, bf16[8,6144,1024]{2,1,0:T(8,128)(2,1)} %all-gather.16.cloned.1.call-done), kind=kOutput, calls=%fused_computation.69 | convolution fusion | flops 19327352832 | bytes 37748736 | tf_op jit(solution)/shard_map/dot_general | solution.py:17
  1374.5 28.4 %fusion.78.refs_2_ = bf16[1536,1024]{1,0:T(8,128)(2,1)} fusion(f32[1536,1024]{1,0:T(8,128)S(1)} %fusion.46, bf16[1536,6144]{1,0:T(8,128)(2,1)} %copy-done, bf16[8,6144,1024]{2,1,0:T(8,128)(2,1)} %all-gather.16.cloned.1.call-done), kind=kOutput, calls=%fused_computation.117 | convolution fusion | flops 19343081472 | bytes 40894464 | tf_op jit(solution)/shard_map/dot_general | solution.py:17
  1403.0 23.7 %fusion.44 = f32[1536,1024]{1,0:T(8,128)S(1)} fusion(bf16[1536,6144]{1,0:T(8,128)(2,1)} %copy-done, bf16[8,6144,1024]{2,1,0:T(8,128)(2,1)} %all-gather.16.cloned.1.call-done), kind=kOutput, calls=%fused_computation.65 | convolution fusion | flops 19327352832 | bytes 37748736 | tf_op jit(solution)/shard_map/dot_general | solution.py:17
  1426.7 28.9 %fusion.87.refs_3_ = bf16[1536,1024]{1,0:T(8,128)(2,1)} fusion(f32[1536,1024]{1,0:T(8,128)S(1)} %fusion.44, bf16[1536,6144]{1,0:T(8,128)(2,1)} %copy-done, bf16[8,6144,1024]{2,1,0:T(8,128)(2,1)} %all-gather.16.cloned.1.call-done), kind=kOutput, calls=%fused_computation.126 | convolution fusion | flops 19343081472 | bytes 40894464 | tf_op jit(solution)/shard_map/dot_general | solution.py:17
  1455.6 232.0 %all-gather.18.cloned.1.call-done = bf16[8,6144,1024]{2,1,0:T(8,128)(2,1)} async-done(((bf16[8,768,1024]{2,1,0:T(8,128)(2,1)}), bf16[8,6144,1024]{2,1,0:T(8,128)(2,1)}) %all-gather.18.cloned.1.call-update) | async-done | bytes 100663312 | tf_op jit(solution)/shard_map/all_gather | solution.py:188
  1687.6 23.7 %fusion.42 = f32[1536,1024]{1,0:T(8,128)S(1)} fusion(bf16[1536,6144]{1,0:T(8,128)(2,1)} %copy-done, bf16[8,6144,1024]{2,1,0:T(8,128)(2,1)} %all-gather.18.cloned.1.call-done), kind=kOutput, calls=%fused_computation.61 | convolution fusion | flops 19327352832 | bytes 37748736 | tf_op jit(solution)/shard_map/dot_general | solution.py:17
  1711.3 28.4 %fusion.96.refs_0_ = bf16[1536,1024]{1,0:T(8,128)(2,1)} fusion(f32[1536,1024]{1,0:T(8,128)S(1)} %fusion.42, bf16[1536,6144]{1,0:T(8,128)(2,1)} %copy-done, bf16[8,6144,1024]{2,1,0:T(8,128)(2,1)} %all-gather.18.cloned.1.call-done), kind=kOutput, calls=%fused_computation.135 | convolution fusion | flops 19343081472 | bytes 40894464 | tf_op jit(solution)/shard_map/dot_general | solution.py:17
  1739.7 23.8 %fusion.40 = f32[1536,1024]{1,0:T(8,128)S(1)} fusion(bf16[1536,6144]{1,0:T(8,128)(2,1)} %copy-done, bf16[8,6144,1024]{2,1,0:T(8,128)(2,1)} %all-gather.18.cloned.1.call-done), kind=kOutput, calls=%fused_computation.57 | convolution fusion | flops 19327352832 | bytes 37748736 | tf_op jit(solution)/shard_map/dot_general | solution.py:17
  1763.6 28.5 %fusion.105.refs_1_ = bf16[1536,1024]{1,0:T(8,128)(2,1)} fusion(f32[1536,1024]{1,0:T(8,128)S(1)} %fusion.40, bf16[1536,6144]{1,0:T(8,128)(2,1)} %copy-done, bf16[8,6144,1024]{2,1,0:T(8,128)(2,1)} %all-gather.18.cloned.1.call-done), kind=kOutput, calls=%fused_computation.144 | convolution fusion | flops 19343081472 | bytes 40894464 | tf_op jit(solution)/shard_map/dot_general | solution.py:17
  1792.0 23.7 %fusion.38 = f32[1536,1024]{1,0:T(8,128)S(1)} fusion(bf16[1536,6144]{1,0:T(8,128)(2,1)} %copy-done, bf16[8,6144,1024]{2,1,0:T(8,128)(2,1)} %all-gather.18.cloned.1.call-done), kind=kOutput, calls=%fused_computation.53 | convolution fusion | flops 19327352832 | bytes 37748736 | tf_op jit(solution)/shard_map/dot_general | solution.py:17
  1815.7 28.7 %fusion.114.refs_2_ = bf16[1536,1024]{1,0:T(8,128)(2,1)} fusion(f32[1536,1024]{1,0:T(8,128)S(1)} %fusion.38, bf16[1536,6144]{1,0:T(8,128)(2,1)} %copy-done, bf16[8,6144,1024]{2,1,0:T(8,128)(2,1)} %all-gather.18.cloned.1.call-done), kind=kOutput, calls=%fused_computation.153 | convolution fusion | flops 19343081472 | bytes 40894464 | tf_op jit(solution)/shard_map/dot_general | solution.py:17
  1844.4 23.7 %fusion.36 = f32[1536,1024]{1,0:T(8,128)S(1)} fusion(bf16[1536,6144]{1,0:T(8,128)(2,1)} %copy-done, bf16[8,6144,1024]{2,1,0:T(8,128)(2,1)} %all-gather.18.cloned.1.call-done), kind=kOutput, calls=%fused_computation.49 | convolution fusion | flops 19327352832 | bytes 37748736 | tf_op jit(solution)/shard_map/dot_general | solution.py:17
  1868.1 28.5 %fusion.123.act_ref = bf16[1536,1024]{1,0:T(8,128)(2,1)} fusion(f32[1536,1024]{1,0:T(8,128)S(1)} %fusion.36, bf16[1536,6144]{1,0:T(8,128)(2,1)} %copy-done, bf16[8,6144,1024]{2,1,0:T(8,128)(2,1)} %all-gather.18.cloned.1.call-done), kind=kOutput, calls=%fused_computation.162 | convolution fusion | flops 19343081472 | bytes 40894464 | tf_op jit(solution)/shard_map/dot_general | solution.py:17
  1896.6 19.1 all-gather.24.cloned.1.call-done.refs_4_
  1915.7 92.4 %group_down.2.refs_5_ = f32[1536,6144]{1,0:T(8,128)} custom-call(bf16[1536,1024]{1,0:T(8,128)(2,1)} %fusion.60.refs_0_, bf16[1536,1024]{1,0:T(8,128)(2,1)} %fusion.69.refs_1_, bf16[1536,1024]{1,0:T(8,128)(2,1)} %fusion.78.refs_2_, bf16[1536,1024]{1,0:T(8,128)(2,1)} %fusion.87.refs_3_, bf16[4,1024,6144]{2,1,0:T(8,128)(2,1)} %all-gather.24.cloned.1.call-done.refs_4_, ...), custom_call_target="tpu_custom_call" | custom-call | flops 77309411328 | bytes 75497472 | tf_op jit(solution)/shard_map/group_down/pallas_call | solution.py:97
  2008.1 82.7 %all-gather.22.cloned.1.call-done.refs_3_ = bf16[3,1024,6144]{2,1,0:T(8,128)(2,1)} async-done(((bf16[3,128,6144]{2,1,0:T(8,128)(2,1)}), bf16[3,1024,6144]{2,1,0:T(8,128)(2,1)}) %all-gather.22.cloned.1.call-update) | async-done | bytes 37748752 | tf_op jit(solution)/shard_map/all_gather | solution.py:196
  2090.8 72.9 %group_down.3.acc_ref = f32[1536,6144]{1,0:T(8,128)} custom-call(bf16[1536,1024]{1,0:T(8,128)(2,1)} %fusion.96.refs_0_, bf16[1536,1024]{1,0:T(8,128)(2,1)} %fusion.105.refs_1_, bf16[1536,1024]{1,0:T(8,128)(2,1)} %fusion.114.refs_2_, bf16[3,1024,6144]{2,1,0:T(8,128)(2,1)} %all-gather.22.cloned.1.call-done.refs_3_, f32[1536,3]{1,0:T(8,128)} %slice.183.refs_4_, ...), custom_call_target="tpu_custom_call" | custom-call | flops 57982058496 | bytes 75497472 | tf_op jit(solution)/shard_map/group_down/pallas_call | solution.py:97
  2163.7 41.3 %last_down.1 = bf16[1536,6144]{1,0:T(8,128)(2,1)} custom-call(bf16[1536,1024]{1,0:T(8,128)(2,1)} %fusion.123.act_ref, bf16[1024,6144]{1,0:T(8,128)(2,1)} %bitcast.197, f32[1536,1]{1,0:T(8,128)} %slice.182.comb_ref, f32[1536,6144]{1,0:T(8,128)} %group_down.3.acc_ref, bf16[1536,6144]{1,0:T(8,128)(2,1)} %get-tuple-element.174.mid_ref, f32[1,6144]{1,0:T(1,128)} %convert.25.gain_ref), custom_call_target="tpu_custom_call" | custom-call | flops 19327352832 | bytes 75497472 | tf_op jit(solution)/shard_map/last_down/pallas_call | solution.py:130
  (114 shorter events, 158.6 us)
Async XLA Ops:
  7.2 340.0 %all-gather.10.cloned.1.call-start = ((), (), s32[]{:S(2)}) async-start(), calls=%async_computation | async-start | bytes 84934656 | tf_op jit(solution)/shard_map/all_gather | solution.py:167
  7.9 473.0 %all-gather.12.cloned.1.call-start = ((), (), s32[]{:S(2)}) async-start(), calls=%async_computation.1 | async-start | bytes 28311552 | tf_op jit(solution)/shard_map/all_gather | solution.py:169
  11.9 877.9 %all-gather.14.cloned.1.call-start = ((), (), s32[]{:S(2)}) async-start(), calls=%async_computation.2 | async-start | bytes 84934656 | tf_op jit(solution)/shard_map/all_gather | solution.py:172
  12.6 1233.5 %all-gather.16.cloned.1.call-start = ((), (), s32[]{:S(2)}) async-start(), calls=%async_computation.3 | async-start | bytes 113246208 | tf_op jit(solution)/shard_map/all_gather | solution.py:188
  32.4 1655.2 %all-gather.18.cloned.1.call-start = ((), (), s32[]{:S(2)}) async-start(), calls=%async_computation.4 | async-start | bytes 113246208 | tf_op jit(solution)/shard_map/all_gather | solution.py:188
  42.9 1872.8 %all-gather.24.cloned.1.call-start = ((), (), s32[]{:S(2)}) async-start(), calls=%async_computation.7 | async-start | bytes 56623104 | tf_op jit(solution)/shard_map/all_gather | solution.py:196
  49.1 8.0 copy-start.9
  49.1 8.1 copy-start.11
  49.1 8.3 copy-start.12
  49.1 8.5 copy-start.13
  49.1 8.7 copy-start.14
  49.2 2041.6 %all-gather.22.cloned.1.call-start = ((), (), s32[]{:S(2)}) async-start(), calls=%async_computation.6 | async-start | bytes 42467328 | tf_op jit(solution)/shard_map/all_gather | solution.py:196
  54.3 30.2 %copy-start.10 = (s32[1536,2]{0,1:T(2,128)S(1)}, s32[1536,2]{0,1:T(2,128)}, u32[]{:S(2)}) copy-start(s32[1536,2]{0,1:T(2,128)} %param.19) | copy-start | bytes 36868
  54.3 2109.3 %all-gather.20.cloned.1.call-start = ((), (), s32[]{:S(2)}) async-start(), calls=%async_computation.5 | async-start | bytes 14155776 | tf_op jit(solution)/shard_map/all_gather | solution.py:197
  550.4 16.2 copy-start.4
  550.4 16.2 copy-start.5
  624.6 20.3 copy-start.1
  650.8 20.4 copy-start.15
  889.8 138.5 %copy-start.7 = (f32[1,8,768]{2,0,1:T(1,128)S(1)}, f32[1,8,768]{2,0,1:T(1,128)}, u32[]{:S(2)}) copy-start(f32[1,8,768]{2,0,1:T(1,128)} %get-tuple-element.189) | copy-start | bytes 73732
  1028.2 28.0 %copy-start.8 = (f32[1,8,768]{2,0,1:T(1,128)S(1)}, f32[1,8,768]{2,0,1:T(1,128)}, u32[]{:S(2)}) copy-start(f32[1,8,768]{2,0,1:T(1,128)} %get-tuple-element.188) | copy-start | bytes 73732
  1056.3 18.6 copy-start.6
  1068.0 6.9 copy-start
  1068.0 12.6 copy-start.3
  1081.1 1.2 copy-start.2
Sparse Core Ops, SparseCore 0:
  9.8 337.3 all-gather.9
  349.6 119.6 all-gather.11
  471.1 333.5 all-gather.13
  806.4 439.7 all-gather.15
  1247.9 439.6 all-gather.17
  1689.3 226.3 all-gather.23
  1917.5 173.2 all-gather.21
  2092.6 66.2 all-gather.19
